TPU v7x, 128 devices: a whole 4x4x4 slice. The times are simulated.
128 devices in a mesh: sys: 1, aux: 64 (over z, y, x), orb: 2 (over core).
Axes of the slice: x: 4, y: 4, z: 4, core: 2. Of those that a mesh axis runs over, the one named last changes fastest.
Arguments:
- b_tensor: float32 [1280, 512, 512], P(('sys', 'aux'), 'orb')
- c_alpha: float32 [512, 105], P('sys')
- c_beta: float32 [512, 104], P('sys')
Outputs:
- output 1: float32 [512, 512], P(('sys', 'orb'), 'aux')
- output 2: float32 [512, 512], P(('sys', 'orb'), 'aux')
All inputs are finite; a program needn't handle non-finite values.
Results may differ from a plain program's by a relative error of at most 0.001.
Values are sent between devices in bfloat16 or wider.
A program may use at most 1 GiB of HBM per device.

v0:
```python
import jax
import jax.numpy as jnp
from jax import lax
from jax.sharding import PartitionSpec as P

TOP_PRECISION = lax.Precision.HIGHEST


def solution(mesh):
    orb_count = mesh.shape['orb']
    shift_pairs = [(source, (source + 1) % orb_count) for source in range(orb_count)]

    def pair_product(left, right):
        return jnp.einsum('qmi,qni->mn', left, right, precision=TOP_PRECISION, preferred_element_type=jnp.float32)

    def local_build(b_local, c_alpha, c_beta):
        m_loc = b_local.shape[1]
        n_bas = b_local.shape[2]
        orb_index = lax.axis_index('orb')
        row_start = orb_index * m_loc
        alpha_rows = lax.dynamic_slice_in_dim(c_alpha, row_start, m_loc, 0)
        beta_rows = lax.dynamic_slice_in_dim(c_beta, row_start, m_loc, 0)
        dens_rows = jnp.einsum('mi,si->ms', alpha_rows, c_alpha, precision=TOP_PRECISION, preferred_element_type=jnp.float32) + jnp.einsum('mi,si->ms', beta_rows, c_beta, precision=TOP_PRECISION, preferred_element_type=jnp.float32)
        gamma_part = jnp.einsum('qms,ms->q', b_local, dens_rows, precision=TOP_PRECISION, preferred_element_type=jnp.float32)
        gamma_vec = lax.psum(gamma_part, 'orb')
        coul_part = jnp.einsum('qmn,q->mn', b_local, gamma_vec, precision=TOP_PRECISION, preferred_element_type=jnp.float32)
        half_alpha = jnp.einsum('qml,li->qmi', b_local, c_alpha, precision=TOP_PRECISION, preferred_element_type=jnp.float32)
        half_beta = jnp.einsum('qml,li->qmi', b_local, c_beta, precision=TOP_PRECISION, preferred_element_type=jnp.float32)
        empty_rows = jnp.zeros((m_loc, n_bas), jnp.float32)
        exch_alpha = lax.dynamic_update_slice_in_dim(empty_rows, pair_product(half_alpha, half_alpha), row_start, 1)
        exch_beta = lax.dynamic_update_slice_in_dim(empty_rows, pair_product(half_beta, half_beta), row_start, 1)

        def pass_step(step, carry):
            visit_alpha, visit_beta, acc_alpha, acc_beta = carry
            visit_alpha = lax.ppermute(visit_alpha, 'orb', shift_pairs)
            visit_beta = lax.ppermute(visit_beta, 'orb', shift_pairs)
            col_start = ((orb_index - step) % orb_count) * m_loc
            acc_alpha = lax.dynamic_update_slice_in_dim(acc_alpha, pair_product(half_alpha, visit_alpha), col_start, 1)
            acc_beta = lax.dynamic_update_slice_in_dim(acc_beta, pair_product(half_beta, visit_beta), col_start, 1)
            return visit_alpha, visit_beta, acc_alpha, acc_beta

        loop_out = lax.fori_loop(1, orb_count, pass_step, (half_alpha, half_beta, exch_alpha, exch_beta))
        g_alpha = lax.psum_scatter(coul_part - loop_out[2], 'aux', scatter_dimension=1, tiled=True)
        g_beta = lax.psum_scatter(coul_part - loop_out[3], 'aux', scatter_dimension=1, tiled=True)
        return g_alpha, g_beta

    spec_b = P(('sys', 'aux'), 'orb', None)
    spec_c = P('sys', None)
    spec_g = P(('sys', 'orb'), 'aux')
    return jax.shard_map(local_build, mesh=mesh, in_specs=(spec_b, spec_c, spec_c), out_specs=(spec_g, spec_g), check_vma=False)
```

profile of v0, /device:TPU:0, one launch (start us, length us, event | category | flops | bytes accessed | tf_op | source)
XLA Modules:
  0.0 817.5 jit_solution(8190209917669293464)
XLA Ops:
  7.2 0.0 copy-start
  7.2 0.0 copy-start.2
  7.2 0.0 reduce-scatter.3.cloned.1.call-start
  7.2 0.9 copy-done
  8.1 0.0 copy-start.1
  8.1 14.6 %fusion.13 = f32[20,256,105]{1,2,0:T(8,128)S(1)} fusion(f32[20,256,512]{2,1,0:T(8,128)} %param.3, f32[512,105]{0,1:T(8,128)S(1)} %copy-done), kind=kOutput, calls=%fused_computation.18 | convolution fusion | flops 3303014400 | bytes 12851200 | tf_op jit(solution)/shard_map/qml,li->qmi/dot_general | solution.py:27
  22.7 0.3 collective-permute-start
  23.0 0.0 copy-done.2
  23.0 0.0 copy-done.1
  23.1 11.7 %fusion.15 = f32[20,256,104]{1,2,0:T(8,128)} fusion(f32[20,256,512]{2,1,0:T(8,128)S(1)} %copy-done.1, f32[512,104]{0,1:T(8,128)S(1)} %copy-done.2), kind=kOutput, calls=%fused_computation.20 | convolution fusion | flops 3271557120 | bytes 12828672 | tf_op jit(solution)/shard_map/qml,li->qmi/dot_general | solution.py:28
  34.7 0.7 collective-permute-start.1
  35.4 0.6 fusion.17
  36.1 0.6 fusion.4
  36.7 19.5 %fusion.9 = f32[20]{0:T(128)S(1)} fusion(f32[20,256,512]{2,1,0:T(8,128)} %param.3, f32[256,512,1]{1,0,2:T(8,128)S(1)} %fusion.4), kind=kOutput, calls=%fused_computation.14 | convolution fusion | flops 31457280 | bytes 11010128 | tf_op jit(solution)/shard_map/qms,ms->q/dot_general | solution.py:24
  56.2 2.9 psum.7
  59.1 17.7 %fusion = f32[1,256,512]{2,0,1:T(1,128)} fusion(f32[20,256,512]{2,1,0:T(8,128)} %param.3, f32[20]{0:T(128)S(1)} %psum.7), kind=kOutput, calls=%fused_computation | convolution fusion | flops 31457280 | bytes 11010128 | tf_op jit(solution)/shard_map/qmn,q->mn/dot_general | solution.py:26
  76.8 1.4 copy.11
  78.3 5.9 fusion.8
  84.3 3.9 fusion.6
  88.1 0.0 collective-permute-done.1
  88.2 5.9 fusion.7
  94.1 0.0 collective-permute-done
  94.1 5.7 fusion.5
  99.8 1.1 bitcast_subtract_fusion
  100.9 0.0 reduce-scatter.3.cloned.1.call-update
  100.9 0.0 reduce-scatter.5.cloned.1.call-start
  101.0 0.7 reduce-scatter.5.cloned.1.call-update
  101.7 356.5 %reduce-scatter.3.cloned.1.call-done = f32[256,8]{0,1:T(8,128)} async-done(((f32[256,512]{0,1:T(8,128)}), f32[256,8]{0,1:T(8,128)}) %reduce-scatter.3.cloned.1.call-update) | async-done | bytes 8208 | tf_op jit(solution)/shard_map/reduce_scatter | solution.py:43
  458.2 352.3 %reduce-scatter.5.cloned.1.call-done = f32[256,8]{0,1:T(8,128)} async-done(((f32[256,512]{0,1:T(8,128)}), f32[256,8]{0,1:T(8,128)}) %reduce-scatter.5.cloned.1.call-update) | async-done | bytes 8208 | tf_op jit(solution)/shard_map/reduce_scatter | solution.py:44
  (2 shorter events, 0.1 us)
Async XLA Ops:
  7.2 0.9 copy-start
  7.2 15.9 %copy-start.2 = (f32[512,104]{0,1:T(8,128)S(1)}, f32[512,104]{0,1:T(8,128)}, u32[]{:S(2)}) copy-start(f32[512,104]{0,1:T(8,128)} %param.5) | copy-start | bytes 638980
  7.2 451.0 %reduce-scatter.3.cloned.1.call-start = ((), (), s32[]{:S(2)}) async-start(), calls=%async_computation.2 | async-start | bytes 532480 | tf_op jit(solution)/shard_map/reduce_scatter | solution.py:43
  8.1 14.9 %copy-start.1 = (f32[20,256,512]{2,1,0:T(8,128)S(1)}, f32[20,256,512]{2,1,0:T(8,128)}, u32[]{:S(2)}) copy-start(f32[20,256,512]{2,1,0:T(8,128)} %param.3) | copy-start | bytes 31457284
  22.7 71.3 %collective-permute-start = (f32[20,256,105]{1,2,0:T(8,128)S(1)}, f32[20,256,105]{1,2,0:T(8,128)}, u32[]{:S(2)}, u32[]{:S(2)}) collective-permute-start(f32[20,256,105]{1,2,0:T(8,128)S(1)} %fusion.13), channel_id=1, source_target_pairs={{0,1},{1,0},{2,3},{3,2},{4,5},{5,4},{6,7},{7,6},{8,9},{9,8},{10,11... | collective-permute-start | bytes 6451208 | tf_op jit(solution)/shard_map/while/body/eval_jaxpr/ppermute | solution.py:35
  34.7 53.4 %collective-permute-start.1 = (f32[20,256,104]{1,2,0:T(8,128)}, f32[20,256,104]{1,2,0:T(8,128)}, u32[]{:S(2)}, u32[]{:S(2)}) collective-permute-start(f32[20,256,104]{1,2,0:T(8,128)} %fusion.15), channel_id=1, source_target_pairs={{0,1},{1,0},{2,3},{3,2},{4,5},{5,4},{6,7},{7,6},{8,9},{9,8},{10,11... | collective-permute-start | bytes 6389768 | tf_op jit(solution)/shard_map/while/body/eval_jaxpr/ppermute | solution.py:36
  100.9 709.6 %reduce-scatter.5.cloned.1.call-start = ((), (), s32[]{:S(2)}) async-start(), calls=%async_computation.3 | async-start | bytes 532480 | tf_op jit(solution)/shard_map/reduce_scatter | solution.py:44
Sparse Core Ops, SparseCore 0:
  101.0 357.1 reduce-scatter.2
  461.1 349.3 reduce-scatter.4
where the time goes:
time: 822 us; the launch traced here: 818 us
  waiting for transfers between devices  710 us (86%)
  matrix products  86.1 us (10%)
  between operations  14.4 us (2%)
    reduce_scatter x1, waiting for transfers between devices, local_build(): lax.psum_scatter(coul_part - loop_out[2], 'aux', scatter_dimension=1, til...  357 us
    reduce_scatter x1, waiting for transfers between devices, local_build(): lax.psum_scatter(coul_part - loop_out[3], 'aux', scatter_dimension=1, til...  352 us
    dot_general x4, matrix products, pair_product(): jnp.einsum('qmi,qni->mn', left, right, precision=TOP_PRECISION, preferred...  21.4 us
    dot_general x1, matrix products, local_build(): jnp.einsum('qms,ms->q', b_local, dens_rows, precision=TOP_PRECISION, pref...  19.5 us
    dot_general x1, matrix products, local_build(): jnp.einsum('qmn,q->mn', b_local, gamma_vec, precision=TOP_PRECISION, pref...  17.7 us
  transfers between devices with their start and end apart: 4, of which 2 were waited for; matrix products, arithmetic and copies ran while one was open for 8% of the time, Pallas kernels for 0%

commit v1 on v0

v1 whole, which is shorter than its diff:
```python
import functools

import jax
import jax.numpy as jnp
from jax import lax
from jax.experimental import pallas as pl
from jax.experimental.pallas import tpu as pltpu
from jax.sharding import PartitionSpec as P

MESH = pl.DeviceIdType.MESH
F32 = jnp.float32
BF16 = jnp.bfloat16
NT = (((1,), (1,)), ((), ()))
ORDERS = ((2, 1, 0), (1, 0, 2), (0, 2, 1), (2, 0, 1))


def split3(value):
    high = value.astype(BF16)
    rest = value - high.astype(F32)
    mid = rest.astype(BF16)
    low = (rest - mid.astype(F32)).astype(BF16)
    return high, mid, low


def mm(a, b):
    return jnp.dot(a, b, preferred_element_type=F32)


def mm_nt(a, b):
    return lax.dot_general(a, b, NT, preferred_element_type=F32)


def kernel(n_q, rows, b_ref, ca_ref, cb_ref, o_ref, b_v, c_f, c_s, t_f, t_r, own, oth, j_acc, y_acc, z_acc,
           p_buf, r1, s1, r2, s2, r3, b_sem, t_send, t_recv, ph_send, ph_recv):
    pairs = n_q // 2
    half = rows // 2
    aux = lax.axis_index("aux")
    orb = lax.axis_index("orb")
    coords = (aux // 16, lax.rem(aux // 4, 4), lax.rem(aux, 4))
    strides = (16, 4, 1)
    partner = {"aux": aux, "orb": 1 - orb}

    def peer(axis, dist):
        target = lax.rem(coords[axis] + dist, 4)
        return {"aux": aux + (target - coords[axis]) * strides[axis], "orb": orb}, target

    def b_copy(q):
        return pltpu.make_async_copy(b_ref.at[q], b_v.at[q], b_sem.at[q])

    for q in range(n_q):
        b_copy(q).start()

    barrier = pltpu.get_barrier_semaphore()
    pl.semaphore_signal(barrier, inc=1, device_id=partner, device_id_type=MESH)
    for axis in range(3):
        for dist in (1, 2, 3):
            pl.semaphore_signal(barrier, inc=1, device_id=peer(axis, dist)[0], device_id_type=MESH)

    c_f[...] = jnp.zeros_like(c_f)
    c_f[:, 0:ca_ref.shape[1]] = ca_ref[...]
    c_f[:, 128:128 + cb_ref.shape[1]] = cb_ref[...]
    for k, part in enumerate(split3(c_f[...])):
        c_s[k] = part
    j_acc[...] = jnp.zeros_like(j_acc)
    y_acc[...] = jnp.zeros_like(y_acc)
    z_acc[...] = jnp.zeros_like(z_acc)
    own_row = pl.multiple_of(orb * half, half)
    oth_row = pl.multiple_of((1 - orb) * half, half)

    def t_copy(p):
        block = pl.ds(2 * p, 2)
        return pltpu.make_async_remote_copy(
            src_ref=t_f.at[block], dst_ref=t_r.at[block], send_sem=t_send.at[p], recv_sem=t_recv.at[p],
            device_id=partner, device_id_type=MESH)

    def t_step(p):
        for e in range(2):
            q = 2 * p + e
            b_copy(q).wait()
        for e in range(2):
            q = 2 * p + e
            h, m, l = split3(b_v[q])
            t = (mm(h, c_s[0]) + mm(m, c_s[0]) + mm(l, c_s[0]) + mm(h, c_s[1]) + mm(m, c_s[1]) + mm(h, c_s[2]))
            t_f[q] = t
            for k, part in enumerate(split3(t)):
                for s in range(2):
                    own[p, k, s, :, e * 128:(e + 1) * 128] = part[:, s * 128:(s + 1) * 128]

    def k_step(p):
        for e in range(2):
            q = 2 * p + e
            t = t_r[q]
            g = jnp.sum(t_f[q] * c_f[pl.ds(own_row, half), :] + t * c_f[pl.ds(oth_row, half), :])
            j_acc[...] += g * b_v[q]
            for k, part in enumerate(split3(t)):
                for s in range(2):
                    oth[k, s, :, e * 128:(e + 1) * 128] = part[:, s * 128:(s + 1) * 128]
        for s in range(2):
            wh, wm, wl = own[p, 0, s], own[p, 1, s], own[p, 2, s]
            oh, om, ol = oth[0, s], oth[1, s], oth[2, s]
            y_acc[s] += (mm_nt(wh * 0.5, wh) + mm_nt(wh, wm) + mm_nt(wm * 0.5, wm) + mm_nt(wh, wl))
            z_acc[s] += (mm_nt(oh, wh) + mm_nt(om, wh) + mm_nt(ol, wh) + mm_nt(oh, wm) + mm_nt(om, wm) + mm_nt(oh, wl))

    def first(p, carry):
        t_step(p)
        return carry

    def middle(p, carry):
        t_step(p)
        t_copy(p - 2).wait_recv()
        k_step(p - 2)
        t_copy(p).start()
        return carry

    def last(p, carry):
        t_copy(p).wait_recv()
        k_step(p)
        return carry

    t_step(0)
    pl.semaphore_wait(barrier, 10)
    t_copy(0).start()
    t_step(1)
    t_copy(1).start()
    lax.fori_loop(2, pairs, middle, 0)
    lax.fori_loop(pairs - 2, pairs, last, 0)
    lax.fori_loop(0, pairs, lambda p, carry: (t_copy(p).wait_send(), carry)[1], 0)

    j_own = j_acc[:, pl.ds(own_row, half)]
    j_oth = j_acc[:, pl.ds(oth_row, half)].T
    for s in range(2):
        y = y_acc[s]
        blocks = ((orb, j_own - (y + y.T)), (1 - orb, j_oth - z_acc[s]))
        for h in range(2):
            for where, block in blocks:
                p_buf[2 * s + h, pl.ds(2 * where, 2)] = block[:, h * 128:(h + 1) * 128].reshape(2, 4, 4, 8, 128)

    def ph_copy(phase, unit, dist):
        order = ORDERS[unit]
        device, target = peer(order[phase], dist)
        if phase == 0:
            axes, src, dst = [0, 1, 2], p_buf, r1
        elif phase == 1:
            axes, src, dst = sorted(order[1:]), s1, r2
        else:
            axes, src, dst = [order[2]], s2, r3
        where = tuple(target if a == order[phase] else slice(None) for a in axes)
        return pltpu.make_async_remote_copy(
            src_ref=src.at[(unit,) + where], dst_ref=dst.at[unit, dist - 1],
            send_sem=ph_send.at[phase, unit, dist - 1], recv_sem=ph_recv.at[phase, unit, dist - 1],
            device_id=device, device_id_type=MESH)

    def kept(phase, unit):
        order = ORDERS[unit]
        if phase == 0:
            axes, src = [0, 1, 2], p_buf
        elif phase == 1:
            axes, src = sorted(order[1:]), s1
        else:
            axes, src = [order[2]], s2
        where = tuple(coords[a] if a == order[phase] else slice(None) for a in axes)
        return src[(unit,) + where]

    for unit in range(4):
        for dist in (2, 1, 3):
            ph_copy(0, unit, dist).start()
    for phase in range(3):
        recv = (r1, r2, r3)[phase]
        for unit in range(4):
            for dist in (1, 2, 3):
                ph_copy(phase, unit, dist).wait_recv()
            total = kept(phase, unit) + recv[unit, 0] + recv[unit, 1] + recv[unit, 2]
            if phase < 2:
                (s1, s2)[phase][unit] = total
                for dist in (2, 1, 3):
                    ph_copy(phase + 1, unit, dist).start()
            else:
                s, h = divmod(unit, 2)
                o_ref[s, :, h * 128:(h + 1) * 128] = total
    for phase in range(3):
        for unit in range(4):
            for dist in (1, 2, 3):
                ph_copy(phase, unit, dist).wait_send()


def solution(mesh):
    def local_build(b_local, c_alpha, c_beta):
        n_q, half, rows = b_local.shape
        pairs = n_q // 2
        vmem = pltpu.VMEM
        dma = pltpu.SemaphoreType.DMA
        out = pl.pallas_call(
            functools.partial(kernel, n_q, rows),
            out_shape=jax.ShapeDtypeStruct((2, 8, half), F32),
            in_specs=[pl.BlockSpec(memory_space=pl.ANY), pl.BlockSpec(memory_space=vmem), pl.BlockSpec(memory_space=vmem)],
            out_specs=pl.BlockSpec(memory_space=vmem),
            scratch_shapes=[
                vmem((n_q, half, rows), F32),
                vmem((rows, 256), F32),
                vmem((3, rows, 256), BF16),
                vmem((n_q, half, 256), F32),
                vmem((n_q, half, 256), F32),
                vmem((pairs, 3, 2, half, 256), BF16),
                vmem((3, 2, half, 256), BF16),
                vmem((half, rows), F32),
                vmem((2, half, half), F32),
                vmem((2, half, half), F32),
                vmem((4, 4, 4, 4, 8, 128), F32),
                vmem((4, 3, 4, 4, 8, 128), F32),
                vmem((4, 4, 4, 8, 128), F32),
                vmem((4, 3, 4, 8, 128), F32),
                vmem((4, 4, 8, 128), F32),
                vmem((4, 3, 8, 128), F32),
                dma((n_q,)),
                dma((pairs,)),
                dma((pairs,)),
                dma((3, 4, 3)),
                dma((3, 4, 3)),
            ],
            compiler_params=pltpu.CompilerParams(
                collective_id=0, has_side_effects=True, vmem_limit_bytes=60 * 1024 * 1024),
        )(b_local, c_alpha, c_beta)
        return out[0].T, out[1].T

    spec_b = P(("sys", "aux"), "orb", None)
    spec_c = P("sys", None)
    spec_g = P(("sys", "orb"), "aux")
    return jax.shard_map(local_build, mesh=mesh, in_specs=(spec_b, spec_c, spec_c), out_specs=(spec_g, spec_g), check_vma=False)
```

time: 822 us -> 53.2 us (0.06)
  waiting for transfers between devices: 710 us -> 0 us
  matrix products: 86.1 us -> 0 us
  Pallas kernels: 0 us -> 47.5 us
  between operations: 14.4 us -> 0.64 us
    reduce_scatter x2 -> x0, waiting for transfers between devices: 709 us -> none  [the longest x1 357 us: local_build(): lax.psum_scatter(coul_part - loop_out[2], 'aux', scatter_dimension=1, til...]
    dot_general x10 -> x0, matrix products: 86.1 us -> none  [the longest x4 21.4 us: pair_product(): jnp.einsum('qmi,qni->mn', left, right, precision=TOP_PRECISION, preferred...]
    pallas_call x0 -> x1, Pallas kernels: none -> 47.5 us  [local_build(): pl.pallas_call(functools.partial(kernel, n_q, rows), out_shape=jax.ShapeD...]
  transfers between devices with their start and end apart: 4 -> 0, of which waited for: 2 -> 0; matrix products, arithmetic and copies ran while one was open for 8% -> 0% of each run, Pallas kernels for 0% -> 0%
where the time goes in v1:
time: 53.2 us; the launch traced here: 53 us
  Pallas kernels  47.5 us (89%)
  local copies, waits for them, and re-layouts  4.85 us (9%)
  between operations  0.64 us (1%)
    pallas_call x1, Pallas kernels, local_build(): pl.pallas_call(functools.partial(kernel, n_q, rows), out_shape=jax.ShapeD...  47.5 us
    unnamed x2, local copies, waits for them, and re-layouts  3.53 us
    transpose x1, local copies, waits for them, and re-layouts, local_build(): return (out[0].T, out[1].T)  1.32 us

profile of v1, /device:TPU:0, one launch (start us, length us, event | category | flops | bytes accessed | tf_op | source)
XLA Modules:
  0.0 53.0 jit_solution(15769317962356379480)
XLA Ops:
  0.6 1.8 %copy.5.ca_ref = f32[512,105]{1,0:T(8,128)} copy(f32[512,105]{0,1:T(8,128)} %param.4) | data formatting | bytes 430080 | tf_op args[1]
  2.4 1.8 %copy.6.cb_ref = f32[512,104]{1,0:T(8,128)} copy(f32[512,104]{0,1:T(8,128)} %param.5) | data formatting | bytes 425984 | tf_op args[2]
  4.2 47.5 %shard_map.50 = f32[2,8,256]{2,1,0:T(8,128)} custom-call(f32[20,256,512]{2,1,0:T(8,128)} %b_ref.1, f32[512,105]{1,0:T(8,128)} %copy.5.ca_ref, f32[512,104]{1,0:T(8,128)} %copy.6.cb_ref), custom_call_target="tpu_custom_call" | custom-call | tf_op jit(solution)/shard_map/pallas_call | solution.py:192
  51.7 1.3 %slice_bitcast_fusion = (f32[256,8]{0,1:T(8,128)}, f32[256,8]{0,1:T(8,128)}) fusion(f32[2,8,256]{2,1,0:T(8,128)} %shard_map.50), kind=kLoop, calls=%fused_computation | loop fusion | bytes 32768 | tf_op jit(solution)/shard_map/transpose | solution.py:223

commit v2 on v1

v2 whole, which is shorter than its diff:
```python
import functools

import jax
import jax.numpy as jnp
from jax import lax
from jax.experimental import pallas as pl
from jax.experimental.pallas import tpu as pltpu
from jax.sharding import PartitionSpec as P

MESH = pl.DeviceIdType.MESH
F32 = jnp.float32
BF16 = jnp.bfloat16
NT = (((1,), (1,)), ((), ()))
ORDERS = ((2, 1, 0), (1, 2, 0))
T_BLOCK = 2
K_BLOCK = 5


def split3(value):
    high = value.astype(BF16)
    rest = value - high.astype(F32)
    mid = rest.astype(BF16)
    low = (rest - mid.astype(F32)).astype(BF16)
    return high, mid, low


def mm(a, b):
    return jnp.dot(a, b, preferred_element_type=F32)


def mm_nt(a, b):
    return lax.dot_general(a, b, NT, preferred_element_type=F32)


def kernel(n_q, rows, b_ref, ca_ref, cb_ref, o_ref, b_v, ca_v, cb_v, c_pad, c_f, c_s, t_f, t_r, own, oth, j_acc, j_t, y_acc, z_acc,
           p_buf, r1, s1, r2, s2, r3, b_sem, c_sem, t_send, t_recv, send1, recv1, send2, recv2, send3, recv3):
    pairs = n_q // 2
    half = rows // 2
    aux = lax.axis_index("aux")
    orb = lax.axis_index("orb")
    coords = (aux // 16, lax.rem(aux // 4, 4), lax.rem(aux, 4))
    strides = (16, 4, 1)
    partner = {"aux": aux, "orb": 1 - orb}

    def peer(axis, dist):
        target = lax.rem(coords[axis] + dist, 4)
        return {"aux": aux + (target - coords[axis]) * strides[axis], "orb": orb}, target

    def b_copy(p):
        block = pl.ds(2 * p, 2)
        return pltpu.make_async_copy(b_ref.at[block], b_v.at[block], b_sem.at[p])

    c_copies = (pltpu.make_async_copy(ca_ref, ca_v, c_sem.at[0]), pltpu.make_async_copy(cb_ref, cb_v, c_sem.at[1]))
    for copy in c_copies:
        copy.start()
    for p in range(2 * T_BLOCK):
        b_copy(p).start()

    barrier = pltpu.get_barrier_semaphore()
    pl.semaphore_signal(barrier, inc=1, device_id=partner, device_id_type=MESH)
    for axis in range(3):
        for dist in (1, 2, 3):
            pl.semaphore_signal(barrier, inc=1, device_id=peer(axis, dist)[0], device_id_type=MESH)

    c_pad[...] = jnp.zeros_like(c_pad)
    for copy in c_copies:
        copy.wait()
    c_pad[0:ca_v.shape[0], :] = ca_v[...]
    c_pad[128:128 + cb_v.shape[0], :] = cb_v[...]
    c_all = c_pad[...].T
    c_f[...] = c_all
    for k, part in enumerate(split3(c_all)):
        c_s[k] = part
    own_row = pl.multiple_of(orb * half, half)
    oth_row = pl.multiple_of((1 - orb) * half, half)

    def t_copy(p):
        block = pl.ds(2 * p, 2)
        return pltpu.make_async_remote_copy(
            src_ref=t_f.at[block], dst_ref=t_r.at[block], send_sem=t_send.at[p], recv_sem=t_recv.at[p],
            device_id=partner, device_id_type=MESH)

    def t_step(p):
        for e in range(2):
            q = 2 * p + e
            h, m, l = split3(b_v[q])
            t = (mm(h, c_s[0]) + mm(m, c_s[0]) + mm(l, c_s[0]) + mm(h, c_s[1]) + mm(m, c_s[1]) + mm(h, c_s[2]))
            t_f[q] = t
            for k, part in enumerate(split3(t)):
                for s in range(2):
                    own[p, k, s, :, e * 128:(e + 1) * 128] = part[:, s * 128:(s + 1) * 128]

    def t_block(i, carry):
        for j in range(T_BLOCK):
            b_copy(T_BLOCK * i + j).wait()

        @pl.when(i < pairs // T_BLOCK - 2)
        def _():
            for j in range(T_BLOCK):
                b_copy(T_BLOCK * (i + 2) + j).start()

        for j in range(T_BLOCK):
            t_step(T_BLOCK * i + j)

        @pl.when(i == 0)
        def _():
            pl.semaphore_wait(barrier, 10)

        for j in range(T_BLOCK):
            t_copy(T_BLOCK * i + j).start()
        return carry

    lax.fori_loop(0, pairs // T_BLOCK, t_block, 0)

    def take(p, j, s):
        for e in range(2):
            for k, part in enumerate(split3(t_r[2 * p + e, :, s * 128:(s + 1) * 128])):
                oth[j, k, :, e * 128:(e + 1) * 128] = part

    def coulomb(p):
        total = None
        for e in range(2):
            q = 2 * p + e
            g = jnp.sum(t_f[q] * c_f[pl.ds(own_row, half), :] + t_r[q] * c_f[pl.ds(oth_row, half), :])
            term = g * b_v[q]
            total = term if total is None else total + term
        return total

    def own_terms(p, s):
        wh, wm, wl = own[p, 0, s], own[p, 1, s], own[p, 2, s]
        return mm_nt(wh * 0.5, wh) + mm_nt(wh, wm) + mm_nt(wm * 0.5, wm) + mm_nt(wh, wl)

    def oth_terms(p, j, s):
        wh, wm, wl = own[p, 0, s], own[p, 1, s], own[p, 2, s]
        oh, om, ol = oth[j, 0], oth[j, 1], oth[j, 2]
        return mm_nt(oh, wh) + mm_nt(om, wh) + mm_nt(ol, wh) + mm_nt(oh, wm) + mm_nt(om, wm) + mm_nt(oh, wl)

    def add(acc, i, value):
        acc[...] = value + jnp.where(i > 0, acc[...], 0.0)

    def alpha_block(i, carry):
        for j in range(K_BLOCK):
            t_copy(K_BLOCK * i + j).wait_recv()
        for j in range(K_BLOCK):
            take(K_BLOCK * i + j, j, 0)
        add(j_acc, i, sum(coulomb(K_BLOCK * i + j) for j in range(K_BLOCK)))
        add(y_acc, i, sum(own_terms(K_BLOCK * i + j, 0) for j in range(K_BLOCK)))
        add(z_acc, i, sum(oth_terms(K_BLOCK * i + j, j, 0) for j in range(K_BLOCK)))
        return carry

    def beta_oth_block(i, carry):
        for j in range(K_BLOCK):
            take(K_BLOCK * i + j, j, 1)
        add(z_acc, i, sum(oth_terms(K_BLOCK * i + j, j, 1) for j in range(K_BLOCK)))
        return carry

    def beta_own_block(i, carry):
        add(y_acc, i, sum(own_terms(K_BLOCK * i + j, 1) for j in range(K_BLOCK)))
        return carry

    z_pair = (pl.ds(2 * orb, 2), pl.ds(2 * (1 - orb), 2))

    def put(s, part, block):
        for h in range(2):
            p_buf[s, h, z_pair[part]] = block[:, h * 128:(h + 1) * 128].reshape(2, 4, 4, 8, 128)

    def at1(h, where):
        return (slice(None), where) if ORDERS[h][0] == 2 else (where,)

    def copy1(s, h, part, dist):
        device, target = peer(ORDERS[h][0], dist)
        return pltpu.make_async_remote_copy(
            src_ref=p_buf.at[(s, h, z_pair[part]) + at1(h, target)], dst_ref=r1.at[s, h, dist - 1, z_pair[part]],
            send_sem=send1.at[s, h, part, dist - 1], recv_sem=recv1.at[s, h, part, dist - 1],
            device_id=device, device_id_type=MESH)

    def copy2(s, h, dist):
        device, target = peer(ORDERS[h][1], dist)
        return pltpu.make_async_remote_copy(
            src_ref=s1.at[s, h, :, target], dst_ref=r2.at[s, h, dist - 1],
            send_sem=send2.at[s, h, dist - 1], recv_sem=recv2.at[s, h, dist - 1],
            device_id=device, device_id_type=MESH)

    def copy3(s, h, dist):
        device, target = peer(ORDERS[h][2], dist)
        return pltpu.make_async_remote_copy(
            src_ref=s2.at[s, h, target], dst_ref=r3.at[s, h, dist - 1],
            send_sem=send3.at[s, h, dist - 1], recv_sem=recv3.at[s, h, dist - 1],
            device_id=device, device_id_type=MESH)

    dists = (2, 1, 3)

    def start1(s, part):
        for dist in dists:
            for h in range(2):
                copy1(s, h, part, dist).start()

    def finish1(s):
        for part in (1, 0):
            for h in range(2):
                for dist in dists:
                    copy1(s, h, part, dist).wait_recv()
                zs = z_pair[part]
                s1[s, h, zs] = (p_buf[(s, h, zs) + at1(h, coords[ORDERS[h][0]])]
                                + r1[s, h, 0, zs] + r1[s, h, 1, zs] + r1[s, h, 2, zs])
        for dist in dists:
            for h in range(2):
                copy2(s, h, dist).start()

    def finish2(s):
        for h in range(2):
            for dist in dists:
                copy2(s, h, dist).wait_recv()
            s2[s, h] = s1[s, h, :, coords[ORDERS[h][1]]] + r2[s, h, 0] + r2[s, h, 1] + r2[s, h, 2]
        for dist in dists:
            for h in range(2):
                copy3(s, h, dist).start()

    def finish3(s):
        for h in range(2):
            for dist in dists:
                copy3(s, h, dist).wait_recv()
            o_ref[s, :, h * 128:(h + 1) * 128] = s2[s, h, coords[0]] + r3[s, h, 0] + r3[s, h, 1] + r3[s, h, 2]

    blocks = pairs // K_BLOCK
    lax.fori_loop(0, blocks, alpha_block, 0)
    j_t[...] = j_acc[:, pl.ds(oth_row, half)].T
    put(0, 1, j_t[...] - z_acc[...])
    put(0, 0, j_acc[:, pl.ds(own_row, half)] - (y_acc[...] + y_acc[...].T))
    start1(0, 1)
    start1(0, 0)
    lax.fori_loop(0, blocks, beta_oth_block, 0)
    put(1, 1, j_t[...] - z_acc[...])
    start1(1, 1)
    lax.fori_loop(0, blocks, beta_own_block, 0)
    put(1, 0, j_acc[:, pl.ds(own_row, half)] - (y_acc[...] + y_acc[...].T))
    start1(1, 0)
    finish1(0)
    finish1(1)
    finish2(0)
    finish2(1)
    finish3(0)
    finish3(1)
    lax.fori_loop(0, pairs, lambda p, carry: (t_copy(p).wait_send(), carry)[1], 0)
    for s in range(2):
        for h in range(2):
            for dist in dists:
                copy1(s, h, 0, dist).wait_send()
                copy1(s, h, 1, dist).wait_send()
                copy2(s, h, dist).wait_send()
                copy3(s, h, dist).wait_send()


def solution(mesh):
    def local_build(b_local, c_alpha, c_beta):
        n_q, half, rows = b_local.shape
        pairs = n_q // 2
        vmem = pltpu.VMEM
        dma = pltpu.SemaphoreType.DMA
        anywhere = pl.BlockSpec(memory_space=pl.ANY)
        out = pl.pallas_call(
            functools.partial(kernel, n_q, rows),
            out_shape=jax.ShapeDtypeStruct((2, 8, half), F32),
            in_specs=[anywhere, anywhere, anywhere],
            out_specs=pl.BlockSpec(memory_space=vmem),
            scratch_shapes=[
                vmem((n_q, half, rows), F32),
                vmem((c_alpha.shape[1], rows), F32),
                vmem((c_beta.shape[1], rows), F32),
                vmem((256, rows), F32),
                vmem((rows, 256), F32),
                vmem((3, rows, 256), BF16),
                vmem((n_q, half, 256), F32),
                vmem((n_q, half, 256), F32),
                vmem((pairs, 3, 2, half, 256), BF16),
                vmem((K_BLOCK, 3, half, 256), BF16),
                vmem((half, rows), F32),
                vmem((half, half), F32),
                vmem((half, half), F32),
                vmem((half, half), F32),
                vmem((2, 2, 4, 4, 4, 8, 128), F32),
                vmem((2, 2, 3, 4, 4, 8, 128), F32),
                vmem((2, 2, 4, 4, 8, 128), F32),
                vmem((2, 2, 3, 4, 8, 128), F32),
                vmem((2, 2, 4, 8, 128), F32),
                vmem((2, 2, 3, 8, 128), F32),
                dma((pairs,)),
                dma((2,)),
                dma((pairs,)),
                dma((pairs,)),
                dma((2, 2, 2, 3)),
                dma((2, 2, 2, 3)),
                dma((2, 2, 3)),
                dma((2, 2, 3)),
                dma((2, 2, 3)),
                dma((2, 2, 3)),
            ],
            compiler_params=pltpu.CompilerParams(
                collective_id=0, has_side_effects=True, vmem_limit_bytes=60 * 1024 * 1024),
        )(b_local, c_alpha.T, c_beta.T)
        return out[0].T, out[1].T

    spec_b = P(("sys", "aux"), "orb", None)
    spec_c = P("sys", None)
    spec_g = P(("sys", "orb"), "aux")
    return jax.shard_map(local_build, mesh=mesh, in_specs=(spec_b, spec_c, spec_c), out_specs=(spec_g, spec_g), check_vma=False)
```

time: 53.2 us -> 42.9 us (0.81)
  Pallas kernels: 47.5 us -> 40.8 us
  local copies, waits for them, and re-layouts: 4.85 us -> 1.32 us
    pallas_call x1, Pallas kernels: 47.5 us -> 40.8 us  [local_build(): pl.pallas_call(functools.partial(kernel, n_q, rows), out_shape=jax.ShapeD...]
    unnamed x2 -> x0, local copies, waits for them, and re-layouts: 3.53 us -> none
where the time goes in v2:
time: 42.9 us; the launch traced here: 42.8 us
  Pallas kernels  40.8 us (95%)
  local copies, waits for them, and re-layouts  1.32 us (3%)
  between operations  0.64 us (1%)
    pallas_call x1, Pallas kernels, local_build(): pl.pallas_call(functools.partial(kernel, n_q, rows), out_shape=jax.ShapeD...  40.8 us
    transpose x1, local copies, waits for them, and re-layouts, local_build(): return (out[0].T, out[1].T)  1.32 us

profile of v2, /device:TPU:0, one launch (start us, length us, event | category | flops | bytes accessed | tf_op | source)
XLA Modules:
  0.0 42.8 jit_solution(13045925856789783368)
XLA Ops:
  0.6 40.8 %shard_map.50 = f32[2,8,256]{2,1,0:T(8,128)} custom-call(f32[20,256,512]{2,1,0:T(8,128)} %b_ref.1, f32[105,512]{1,0:T(8,128)} %bitcast.10, f32[104,512]{1,0:T(8,128)} %bitcast.11), custom_call_target="tpu_custom_call" | custom-call | tf_op jit(solution)/shard_map/pallas_call | solution.py:261
  41.5 1.3 %slice_bitcast_fusion = (f32[256,8]{0,1:T(8,128)}, f32[256,8]{0,1:T(8,128)}) fusion(f32[2,8,256]{2,1,0:T(8,128)} %shard_map.50), kind=kLoop, calls=%fused_computation | loop fusion | bytes 32768 | tf_op jit(solution)/shard_map/transpose | solution.py:301

commit v3 on v2

v3 whole, which is shorter than its diff:
```python
import functools

import jax
import jax.numpy as jnp
from jax import lax
from jax.experimental import pallas as pl
from jax.experimental.pallas import tpu as pltpu
from jax.sharding import PartitionSpec as P

MESH = pl.DeviceIdType.MESH
F32 = jnp.float32
BF16 = jnp.bfloat16
NT = (((1,), (1,)), ((), ()))
T_BLOCK = 5
X_FIRST, Y_FIRST, Z_FIRST = (2, 0, 1), (1, 0, 2), (0, 1, 2)
ORDERS = (((X_FIRST, Y_FIRST), (Y_FIRST, X_FIRST)), ((Z_FIRST, X_FIRST), (Y_FIRST, Z_FIRST)))


def split3(value):
    high = value.astype(BF16)
    rest = value - high.astype(F32)
    mid = rest.astype(BF16)
    low = (rest - mid.astype(F32)).astype(BF16)
    return high, mid, low


def mm(a, b):
    return jnp.dot(a, b, preferred_element_type=F32)


def mm_nt(a, b):
    return lax.dot_general(a, b, NT, preferred_element_type=F32)


def joined(ref):
    return jnp.concatenate([ref[i] for i in range(ref.shape[0])], axis=1)


def kernel(n_q, rows, *refs):
    (b_ref, ca_ref, cb_ref, o_ref, b_v, ca_v, cb_v, c_pad, c_f, c_s, t_f, t_r, g_f, g_r, own, oth, j_acc, j_t, y_acc, z_f, z_r,
     p_buf, r1, s1, r2, s2, r3, b_sem, c_sem, t_send, t_recv, g_send, g_recv, z_send, z_recv,
     send1, recv1, send2, recv2, send3, recv3) = refs
    pairs = n_q // 2
    shared = pairs // 2
    half = rows // 2
    aux = lax.axis_index("aux")
    orb = lax.axis_index("orb")
    coords = (aux // 16, lax.rem(aux // 4, 4), lax.rem(aux, 4))
    strides = (16, 4, 1)
    partner = {"aux": aux, "orb": 1 - orb}

    def peer(axis, dist):
        target = lax.rem(coords[axis] + dist, 4)
        return {"aux": aux + (target - coords[axis]) * strides[axis], "orb": orb}, target

    def b_copy(p):
        first = shared * (1 - orb)
        where = lax.rem(p + first, pairs)
        return pltpu.make_async_copy(b_ref.at[pl.ds(2 * where, 2)], b_v.at[pl.ds(2 * p, 2)], b_sem.at[p])

    c_copies = (pltpu.make_async_copy(ca_ref, ca_v, c_sem.at[0]), pltpu.make_async_copy(cb_ref, cb_v, c_sem.at[1]))
    for copy in c_copies:
        copy.start()
    for p in range(T_BLOCK):
        b_copy(p).start()

    barrier = pltpu.get_barrier_semaphore()
    pl.semaphore_signal(barrier, inc=1, device_id=partner, device_id_type=MESH)
    for axis in range(3):
        for dist in (1, 2, 3):
            pl.semaphore_signal(barrier, inc=1, device_id=peer(axis, dist)[0], device_id_type=MESH)

    c_pad[...] = jnp.zeros_like(c_pad)
    for copy in c_copies:
        copy.wait()
    c_pad[0:ca_v.shape[0], :] = ca_v[...]
    c_pad[128:128 + cb_v.shape[0], :] = cb_v[...]
    c_all = c_pad[...].T
    c_f[...] = c_all
    for k, part in enumerate(split3(c_all)):
        c_s[k, 0] = part[:, 0:128]
        c_s[k, 1] = part[:, 128:256]
    own_row = pl.multiple_of(orb * half, half)
    oth_row = pl.multiple_of((1 - orb) * half, half)

    def t_copy(p):
        return pltpu.make_async_remote_copy(
            src_ref=t_f.at[p], dst_ref=t_r.at[p], send_sem=t_send.at[p], recv_sem=t_recv.at[p],
            device_id=partner, device_id_type=MESH)

    def g_copy(p):
        there = lax.rem(p + shared, pairs)
        return pltpu.make_async_remote_copy(
            src_ref=g_f.at[p], dst_ref=g_r.at[there], send_sem=g_send.at[p], recv_sem=g_recv.at[there],
            device_id=partner, device_id_type=MESH)

    def g_landed(p):
        g_copy(lax.rem(p + shared, pairs)).wait_recv()

    def z_copy(s):
        return pltpu.make_async_remote_copy(
            src_ref=z_f.at[s], dst_ref=z_r.at[s], send_sem=z_send.at[s], recv_sem=z_recv.at[s],
            device_id=partner, device_id_type=MESH)

    def t_step(p):
        for e in range(2):
            h, m, l = split3(b_v[2 * p + e])
            ch, cm, cl = joined(c_s.at[0]), joined(c_s.at[1]), joined(c_s.at[2])
            t = mm(h, ch) + mm(m, ch) + mm(l, ch) + mm(h, cm) + mm(m, cm) + mm(h, cl)
            t_f[p, e] = t
            prod = (t * c_f[pl.ds(own_row, half), :]).reshape(half // 8, 8, 256).sum(axis=0)
            g_f[p, e] = prod[:, 0:128] + prod[:, 128:256]
            for k, part in enumerate(split3(t)):
                for s in range(2):
                    own[p, k, s, e] = part[:, s * 128:(s + 1) * 128]

    def send_t(p):
        g_copy(p).start()

        @pl.when(p < shared)
        def _():
            t_copy(p).start()

    def t_block(i, carry):
        p = T_BLOCK * i

        @pl.when(i == 0)
        def _():
            for j in range(T_BLOCK, pairs):
                b_copy(j).start()

        for j in range(T_BLOCK):
            b_copy(p + j).wait()
            t_step(p + j)

        @pl.when(i == 0)
        def _():
            pl.semaphore_wait(barrier, 10)

        for j in range(T_BLOCK):
            send_t(p + j)
        return carry

    lax.fori_loop(0, pairs // T_BLOCK, t_block, 0)

    def take(s):
        for j in range(shared):
            for e in range(2):
                for k, part in enumerate(split3(t_r[j, e, :, s * 128:(s + 1) * 128])):
                    oth[s, j, k, e] = part

    def coulomb():
        g = [jnp.sum(g_f[q // 2, q % 2] + g_r[q // 2, q % 2]) for q in range(n_q)]
        for row in range(0, half, 8):
            total = g[0] * b_v[0, row:row + 8, :]
            for q in range(1, n_q):
                total = total + g[q] * b_v[q, row:row + 8, :]
            j_acc[row:row + 8, :] = total

    def own_sum(s, ps):
        total = None
        for p in ps:
            wh, wm, wl = (joined(own.at[p, k, s]) for k in range(3))
            term = mm_nt(wh * 0.5, wh) + mm_nt(wm, wh) + mm_nt(wl, wh) + mm_nt(wm * 0.5, wm)
            total = term if total is None else total + term
        return total

    def oth_sum(s, work):
        total = None
        for j, parts in work:
            for k in parts:
                right = joined(own.at[shared + j, k, s])
                for lhs in range(3 - k):
                    term = mm_nt(joined(oth.at[s, j, lhs]), right)
                    total = term if total is None else total + term
        return total

    def own_products(s):
        return own_sum(s, range(pairs))

    def oth_products(s):
        return oth_sum(s, [(j, (0, 1, 2)) for j in range(shared)])

    def block(body):
        def trip(_, carry):
            body()
            return carry
        lax.fori_loop(orb, orb + 1, trip, 0)

    z_pair = (pl.ds(2 * orb, 2), pl.ds(2 * (1 - orb), 2))

    def put(s, part, block):
        for h in range(2):
            p_buf[s, h, z_pair[part]] = block[:, h * 128:(h + 1) * 128].reshape(2, 4, 4, 8, 128)

    def put_own(s):
        put(s, 0, j_acc[:, pl.ds(own_row, half)] - (y_acc[...] + y_acc[...].T))

    def put_oth(s):
        put(s, 1, j_t[...] - z_f[s] - z_r[s].T)

    def by_core(body, *args):
        for r in range(2):
            @pl.when(orb == r)
            def _():
                body(r, *args)

    dists = (2, 1, 3)

    def line1(axis, zs, where):
        return {0: (where,), 1: (zs, where), 2: (zs, slice(None), where)}[axis]

    def copy1(r, s, h, part, dist):
        axis = ORDERS[r][s][h][0]
        zs = pl.ds(2 * (r if part == 0 else 1 - r), 2)
        device, target = peer(axis, dist)
        dst = r1.at[s, h, dist - 1] if axis == 0 else r1.at[s, h, dist - 1, zs]
        return pltpu.make_async_remote_copy(
            src_ref=p_buf.at[(s, h) + line1(axis, zs, target)], dst_ref=dst,
            send_sem=send1.at[s, h, part, dist - 1], recv_sem=recv1.at[s, h, part, dist - 1],
            device_id=device, device_id_type=MESH)

    def copy2(r, s, h, dist):
        order = ORDERS[r][s][h]
        device, target = peer(order[1], dist)
        where = (target,) if order[1] == min(order[1:]) else (slice(None), target)
        return pltpu.make_async_remote_copy(
            src_ref=s1.at[(s, h) + where], dst_ref=r2.at[s, h, dist - 1],
            send_sem=send2.at[s, h, dist - 1], recv_sem=recv2.at[s, h, dist - 1],
            device_id=device, device_id_type=MESH)

    def copy3(r, s, h, dist):
        device, target = peer(ORDERS[r][s][h][2], dist)
        return pltpu.make_async_remote_copy(
            src_ref=s2.at[s, h, target], dst_ref=r3.at[s, h, dist - 1],
            send_sem=send3.at[s, h, dist - 1], recv_sem=recv3.at[s, h, dist - 1],
            device_id=device, device_id_type=MESH)

    def start1(r, s, part):
        for dist in dists:
            for h in range(2):
                if ORDERS[r][s][h][0] == 0:
                    @pl.when((peer(0, dist)[1] // 2 == r) == (part == 0))
                    def _():
                        copy1(r, s, h, 0, dist).start()
                else:
                    copy1(r, s, h, part, dist).start()

    def parts1(r, s, h):
        return (0,) if ORDERS[r][s][h][0] == 0 else (1, 0)

    def finish1(r, s):
        for h in range(2):
            axis = ORDERS[r][s][h][0]
            for part in parts1(r, s, h):
                for dist in dists:
                    copy1(r, s, h, part, dist).wait_recv()
                zs = pl.ds(2 * (r if part == 0 else 1 - r), 2)
                kept = p_buf[(s, h) + line1(axis, zs, coords[axis])]
                if axis == 0:
                    s1[s, h] = kept + r1[s, h, 0] + r1[s, h, 1] + r1[s, h, 2]
                else:
                    s1[s, h, zs] = kept + r1[s, h, 0, zs] + r1[s, h, 1, zs] + r1[s, h, 2, zs]
            for dist in dists:
                copy2(r, s, h, dist).start()

    def finish2(r, s):
        for h in range(2):
            order = ORDERS[r][s][h]
            for dist in dists:
                copy2(r, s, h, dist).wait_recv()
            where = (coords[order[1]],) if order[1] == min(order[1:]) else (slice(None), coords[order[1]])
            s2[s, h] = s1[(s, h) + where] + r2[s, h, 0] + r2[s, h, 1] + r2[s, h, 2]
            for dist in dists:
                copy3(r, s, h, dist).start()

    def finish3(r, s):
        for h in range(2):
            for dist in dists:
                copy3(r, s, h, dist).wait_recv()
            o_ref[s, :, h * 128:(h + 1) * 128] = (
                s2[s, h, coords[ORDERS[r][s][h][2]]] + r3[s, h, 0] + r3[s, h, 1] + r3[s, h, 2])

    def sent(r):
        for s in range(2):
            for h in range(2):
                for dist in dists:
                    for part in parts1(r, s, h):
                        copy1(r, s, h, part, dist).wait_send()
                    copy2(r, s, h, dist).wait_send()
                    copy3(r, s, h, dist).wait_send()

    def reduce_rest(r):
        for s in range(2):
            finish1(r, s)
        for s in range(2):
            finish2(r, s)
        for s in range(2):
            finish3(r, s)
        sent(r)

    def alpha_oth():
        take(0)
        z_f[0] = oth_products(0)
        take(1)

    def beta_oth():
        z_f[1] = oth_products(1)
        coulomb()

    def alpha_own():
        y_acc[...] = own_products(0)

    def beta_own():
        y_acc[...] = own_products(1)

    for p in range(shared):
        t_copy(p).wait_recv()
    block(alpha_oth)
    z_copy(0).start()
    for p in range(pairs):
        g_landed(p)
    block(beta_oth)
    z_copy(1).start()
    z_copy(0).wait_recv()
    j_t[...] = j_acc[:, pl.ds(oth_row, half)].T
    put_oth(0)
    by_core(start1, 0, 1)
    block(alpha_own)
    put_own(0)
    by_core(start1, 0, 0)
    z_copy(1).wait_recv()
    put_oth(1)
    by_core(start1, 1, 1)
    block(beta_own)
    put_own(1)
    by_core(start1, 1, 0)
    by_core(reduce_rest)
    for p in range(shared):
        t_copy(p).wait_send()
    for p in range(pairs):
        g_copy(p).wait_send()
    for s in range(2):
        z_copy(s).wait_send()


def solution(mesh):
    def local_build(b_local, c_alpha, c_beta):
        n_q, half, rows = b_local.shape
        pairs = n_q // 2
        vmem = pltpu.VMEM
        dma = pltpu.SemaphoreType.DMA
        anywhere = pl.BlockSpec(memory_space=pl.ANY)
        out = pl.pallas_call(
            functools.partial(kernel, n_q, rows),
            out_shape=jax.ShapeDtypeStruct((2, 8, half), F32),
            in_specs=[anywhere, anywhere, anywhere],
            out_specs=pl.BlockSpec(memory_space=vmem),
            scratch_shapes=[
                vmem((n_q, half, rows), F32),
                vmem((c_alpha.shape[1], rows), F32),
                vmem((c_beta.shape[1], rows), F32),
                vmem((256, rows), F32),
                vmem((rows, 256), F32),
                vmem((3, 2, rows, 128), BF16),
                vmem((pairs, 2, half, 256), F32),
                vmem((pairs // 2, 2, half, 256), F32),
                vmem((pairs, 2, 8, 128), F32),
                vmem((pairs, 2, 8, 128), F32),
                vmem((pairs, 3, 2, 2, half, 128), BF16),
                vmem((2, pairs // 2, 3, 2, half, 128), BF16),
                vmem((half, rows), F32),
                vmem((half, half), F32),
                vmem((half, half), F32),
                vmem((2, half, half), F32),
                vmem((2, half, half), F32),
                vmem((2, 2, 4, 4, 4, 8, 128), F32),
                vmem((2, 2, 3, 4, 4, 8, 128), F32),
                vmem((2, 2, 4, 4, 8, 128), F32),
                vmem((2, 2, 3, 4, 8, 128), F32),
                vmem((2, 2, 4, 8, 128), F32),
                vmem((2, 2, 3, 8, 128), F32),
                dma((pairs,)),
                dma((2,)),
                dma((pairs // 2,)),
                dma((pairs // 2,)),
                dma((pairs,)),
                dma((pairs,)),
                dma((2,)),
                dma((2,)),
                dma((2, 2, 2, 3)),
                dma((2, 2, 2, 3)),
                dma((2, 2, 3)),
                dma((2, 2, 3)),
                dma((2, 2, 3)),
                dma((2, 2, 3)),
            ],
            compiler_params=pltpu.CompilerParams(
                collective_id=0, has_side_effects=True, vmem_limit_bytes=60 * 1024 * 1024),
        )(b_local, c_alpha.T, c_beta.T)
        return out[0].T, out[1].T

    spec_b = P(("sys", "aux"), "orb", None)
    spec_c = P("sys", None)
    spec_g = P(("sys", "orb"), "aux")
    return jax.shard_map(local_build, mesh=mesh, in_specs=(spec_b, spec_c, spec_c), out_specs=(spec_g, spec_g), check_vma=False)
```

time: 42.9 us -> 40.2 us (0.937)
  Pallas kernels: 40.8 us -> 38.1 us
    pallas_call x1, Pallas kernels: 40.8 us -> 38.1 us  [local_build(): pl.pallas_call(functools.partial(kernel, n_q, rows), out_shape=jax.ShapeD...]
where the time goes in v3:
time: 40.2 us; the launch traced here: 40 us
  Pallas kernels  38.1 us (95%)
  local copies, waits for them, and re-layouts  1.32 us (3%)
  between operations  0.64 us (2%)
    pallas_call x1, Pallas kernels, local_build(): pl.pallas_call(functools.partial(kernel, n_q, rows), out_shape=jax.ShapeD...  38.1 us
    transpose x1, local copies, waits for them, and re-layouts, local_build(): return (out[0].T, out[1].T)  1.32 us

profile of v3, /device:TPU:0, one launch (start us, length us, event | category | flops | bytes accessed | tf_op | source)
XLA Modules:
  0.0 40.0 jit_solution(17546983790046877454)
XLA Ops:
  0.6 38.1 %shard_map.50 = f32[2,8,256]{2,1,0:T(8,128)} custom-call(f32[20,256,512]{2,1,0:T(8,128)} %refs_0_.1, f32[105,512]{1,0:T(8,128)} %bitcast.10, f32[104,512]{1,0:T(8,128)} %bitcast.11), custom_call_target="tpu_custom_call" | custom-call | tf_op jit(solution)/shard_map/pallas_call | solution.py:354
  38.7 1.3 %slice_bitcast_fusion = (f32[256,8]{0,1:T(8,128)}, f32[256,8]{0,1:T(8,128)}) fusion(f32[2,8,256]{2,1,0:T(8,128)} %shard_map.50), kind=kLoop, calls=%fused_computation | loop fusion | bytes 32768 | tf_op jit(solution)/shard_map/transpose | solution.py:401

commit v4 on v3

--- a/solution.py
+++ b/solution.py
@@ -353,7 +353,7 @@
         anywhere = pl.BlockSpec(memory_space=pl.ANY)
         out = pl.pallas_call(
             functools.partial(kernel, n_q, rows),
-            out_shape=jax.ShapeDtypeStruct((2, 8, half), F32),
+            out_shape=pltpu.VMEM((2, 8, half), F32),
             in_specs=[anywhere, anywhere, anywhere],
             out_specs=pl.BlockSpec(memory_space=vmem),
             scratch_shapes=[

time: 40.2 us -> 38.8 us (0.965)
  local copies, waits for them, and re-layouts: 1.32 us -> 0.61 us
  Pallas kernels: 38.1 us -> 37.5 us
    transpose x1, local copies, waits for them, and re-layouts: 1.32 us -> 0.61 us  [local_build(): return (out[0].T, out[1].T)]
    pallas_call x1, Pallas kernels: 38.1 us -> 37.5 us  [local_build(): pl.pallas_call(functools.partial(kernel, n_q, rows), out_shape=pltpu.VMEM...]
where the time goes in v4:
time: 38.8 us; the launch traced here: 38.7 us
  Pallas kernels  37.5 us (97%)
  between operations  0.64 us (2%)
  local copies, waits for them, and re-layouts  0.61 us (2%)
    pallas_call x1, Pallas kernels, local_build(): pl.pallas_call(functools.partial(kernel, n_q, rows), out_shape=pltpu.VMEM...  37.5 us

profile of v4, /device:TPU:0, one launch (start us, length us, event | category | flops | bytes accessed | tf_op | source)
XLA Modules:
  0.0 38.7 jit_solution(13028033523098492671)
XLA Ops:
  0.6 37.5 %shard_map.50 = f32[2,8,256]{2,1,0:T(8,128)S(1)} custom-call(f32[20,256,512]{2,1,0:T(8,128)} %refs_0_.1, f32[105,512]{1,0:T(8,128)} %bitcast.10, f32[104,512]{1,0:T(8,128)} %bitcast.11), custom_call_target="tpu_custom_call" | custom-call | tf_op jit(solution)/shard_map/pallas_call | solution.py:354
  38.1 0.6 %slice_bitcast_fusion = (f32[256,8]{0,1:T(8,128)}, f32[256,8]{0,1:T(8,128)}) fusion(f32[2,8,256]{2,1,0:T(8,128)S(1)} %shard_map.50), kind=kLoop, calls=%fused_computation | loop fusion | bytes 32768 | tf_op jit(solution)/shard_map/transpose | solution.py:401

commit v5 on v4

--- a/solution.py
+++ b/solution.py
@@ -11,7 +11,7 @@
 F32 = jnp.float32
 BF16 = jnp.bfloat16
 NT = (((1,), (1,)), ((), ()))
-T_BLOCK = 5
+T_BLOCKS = (1, 4, 5)
 X_FIRST, Y_FIRST, Z_FIRST = (2, 0, 1), (1, 0, 2), (0, 1, 2)
 ORDERS = (((X_FIRST, Y_FIRST), (Y_FIRST, X_FIRST)), ((Z_FIRST, X_FIRST), (Y_FIRST, Z_FIRST)))
 
@@ -61,7 +61,7 @@
     c_copies = (pltpu.make_async_copy(ca_ref, ca_v, c_sem.at[0]), pltpu.make_async_copy(cb_ref, cb_v, c_sem.at[1]))
     for copy in c_copies:
         copy.start()
-    for p in range(T_BLOCK):
+    for p in range(T_BLOCKS[0] + T_BLOCKS[1]):
         b_copy(p).start()
 
     barrier = pltpu.get_barrier_semaphore()
@@ -117,31 +117,24 @@
     def send_t(p):
         g_copy(p).start()
 
-        @pl.when(p < shared)
-        def _():
+        if p < shared:
             t_copy(p).start()
 
-    def t_block(i, carry):
-        p = T_BLOCK * i
-
-        @pl.when(i == 0)
-        def _():
-            for j in range(T_BLOCK, pairs):
-                b_copy(j).start()
-
-        for j in range(T_BLOCK):
-            b_copy(p + j).wait()
-            t_step(p + j)
-
-        @pl.when(i == 0)
-        def _():
+    start = 0
+    for i, size in enumerate(T_BLOCKS):
+        ps = range(start, start + size)
+        start += size
+        for p in ps:
+            b_copy(p).wait()
+        if i == 0:
+            for p in range(T_BLOCKS[0] + T_BLOCKS[1], pairs):
+                b_copy(p).start()
+        for p in ps:
+            t_step(p)
+        if i == 0:
             pl.semaphore_wait(barrier, 10)
-
-        for j in range(T_BLOCK):
-            send_t(p + j)
-        return carry
-
-    lax.fori_loop(0, pairs // T_BLOCK, t_block, 0)
+        for p in ps:
+            send_t(p)
 
     def take(s):
         for j in range(shared):
@@ -149,13 +142,17 @@
                 for k, part in enumerate(split3(t_r[j, e, :, s * 128:(s + 1) * 128])):
                     oth[s, j, k, e] = part
 
-    def coulomb():
-        g = [jnp.sum(g_f[q // 2, q % 2] + g_r[q // 2, q % 2]) for q in range(n_q)]
+    def coulomb(ps, cols, width, old=None):
+        qs = [(p, e) for p in ps for e in range(2)]
+        g = [jnp.sum(g_f[q] + g_r[q]) for q in qs]
+        out = []
         for row in range(0, half, 8):
-            total = g[0] * b_v[0, row:row + 8, :]
-            for q in range(1, n_q):
-                total = total + g[q] * b_v[q, row:row + 8, :]
-            j_acc[row:row + 8, :] = total
+            total = None if old is None else old[row:row + 8, :]
+            for gq, (p, e) in zip(g, qs):
+                term = gq * b_v[2 * p + e, row:row + 8, pl.ds(cols, width)]
+                total = term if total is None else total + term
+            out.append(total)
+        return jnp.concatenate(out, axis=0)
 
     def own_sum(s, ps):
         total = None
@@ -194,10 +191,10 @@
             p_buf[s, h, z_pair[part]] = block[:, h * 128:(h + 1) * 128].reshape(2, 4, 4, 8, 128)
 
     def put_own(s):
-        put(s, 0, j_acc[:, pl.ds(own_row, half)] - (y_acc[...] + y_acc[...].T))
+        put(s, 0, j_acc[...] - (y_acc[...] + y_acc[...].T))
 
     def put_oth(s):
-        put(s, 1, j_t[...] - z_f[s] - z_r[s].T)
+        put(s, 1, -(z_f[s] + z_r[s].T))
 
     def by_core(body, *args):
         for r in range(2):
@@ -299,14 +296,18 @@
             finish3(r, s)
         sent(r)
 
+    kept = range(shared, pairs)
+
     def alpha_oth():
         take(0)
-        z_f[0] = oth_products(0)
+        j_t[...] = coulomb(kept, oth_row, half).T
+        j_acc[...] = coulomb(kept, own_row, half)
+        z_f[0] = oth_products(0) - j_t[...]
+
+    def beta_oth():
         take(1)
-
-    def beta_oth():
-        z_f[1] = oth_products(1)
-        coulomb()
+        j_acc[...] = coulomb(range(shared), own_row, half, j_acc)
+        z_f[1] = oth_products(1) - j_t[...]
 
     def alpha_own():
         y_acc[...] = own_products(0)
@@ -316,14 +317,14 @@
 
     for p in range(shared):
         t_copy(p).wait_recv()
+        g_landed(shared + p)
     block(alpha_oth)
     z_copy(0).start()
-    for p in range(pairs):
+    for p in range(shared):
         g_landed(p)
     block(beta_oth)
     z_copy(1).start()
     z_copy(0).wait_recv()
-    j_t[...] = j_acc[:, pl.ds(oth_row, half)].T
     put_oth(0)
     by_core(start1, 0, 1)
     block(alpha_own)
@@ -369,7 +370,7 @@
                 vmem((pairs, 2, 8, 128), F32),
                 vmem((pairs, 3, 2, 2, half, 128), BF16),
                 vmem((2, pairs // 2, 3, 2, half, 128), BF16),
-                vmem((half, rows), F32),
+                vmem((half, half), F32),
                 vmem((half, half), F32),
                 vmem((half, half), F32),
                 vmem((2, half, half), F32),

time: 38.8 us -> 37.7 us (0.972)
  Pallas kernels: 37.5 us -> 36.3 us
    pallas_call x1, Pallas kernels: 37.5 us -> 36.3 us  [local_build(): pl.pallas_call(functools.partial(kernel, n_q, rows), out_shape=pltpu.VMEM...]
where the time goes in v5:
time: 37.7 us; the launch traced here: 37.5 us
  Pallas kernels  36.3 us (96%)
  between operations  0.64 us (2%)
  local copies, waits for them, and re-layouts  0.61 us (2%)
    pallas_call x1, Pallas kernels, local_build(): pl.pallas_call(functools.partial(kernel, n_q, rows), out_shape=pltpu.VMEM...  36.3 us

profile of v5, /device:TPU:0, one launch (start us, length us, event | category | flops | bytes accessed | tf_op | source)
XLA Modules:
  0.0 37.5 jit_solution(7105908452652159697)
XLA Ops:
  0.6 36.3 %shard_map.50 = f32[2,8,256]{2,1,0:T(8,128)S(1)} custom-call(f32[20,256,512]{2,1,0:T(8,128)} %refs_0_.1, f32[105,512]{1,0:T(8,128)} %bitcast.10, f32[104,512]{1,0:T(8,128)} %bitcast.11), custom_call_target="tpu_custom_call" | custom-call | tf_op jit(solution)/shard_map/pallas_call | solution.py:355
  36.9 0.6 %slice_bitcast_fusion = (f32[256,8]{0,1:T(8,128)}, f32[256,8]{0,1:T(8,128)}) fusion(f32[2,8,256]{2,1,0:T(8,128)S(1)} %shard_map.50), kind=kLoop, calls=%fused_computation | loop fusion | bytes 32768 | tf_op jit(solution)/shard_map/transpose | solution.py:402

commit v6 on v5

--- a/solution.py
+++ b/solution.py
@@ -13,7 +13,7 @@
 NT = (((1,), (1,)), ((), ()))
 T_BLOCKS = (1, 4, 5)
 X_FIRST, Y_FIRST, Z_FIRST = (2, 0, 1), (1, 0, 2), (0, 1, 2)
-ORDERS = (((X_FIRST, Y_FIRST), (Y_FIRST, X_FIRST)), ((Z_FIRST, X_FIRST), (Y_FIRST, Z_FIRST)))
+ORDERS = (((Z_FIRST, X_FIRST), (X_FIRST, Y_FIRST)), ((Y_FIRST, X_FIRST), (Z_FIRST, Y_FIRST)))
 
 
 def split3(value):
@@ -37,7 +37,7 @@
 
 
 def kernel(n_q, rows, *refs):
-    (b_ref, ca_ref, cb_ref, o_ref, b_v, ca_v, cb_v, c_pad, c_f, c_s, t_f, t_r, g_f, g_r, own, oth, j_acc, j_t, y_acc, z_f, z_r,
+    (b_ref, ca_ref, cb_ref, o_ref, b_v, ca_v, cb_v, c_pad, c_f, c_s, t_f, t_r, g_f, g_r, own, oth, j_acc, z_f, z_r,
      p_buf, r1, s1, r2, s2, r3, b_sem, c_sem, t_send, t_recv, g_send, g_recv, z_send, z_recv,
      send1, recv1, send2, recv2, send3, recv3) = refs
     pairs = n_q // 2
@@ -190,9 +190,6 @@
         for h in range(2):
             p_buf[s, h, z_pair[part]] = block[:, h * 128:(h + 1) * 128].reshape(2, 4, 4, 8, 128)
 
-    def put_own(s):
-        put(s, 0, j_acc[...] - (y_acc[...] + y_acc[...].T))
-
     def put_oth(s):
         put(s, 1, -(z_f[s] + z_r[s].T))
 
@@ -278,71 +275,69 @@
             o_ref[s, :, h * 128:(h + 1) * 128] = (
                 s2[s, h, coords[ORDERS[r][s][h][2]]] + r3[s, h, 0] + r3[s, h, 1] + r3[s, h, 2])
 
-    def sent(r):
-        for s in range(2):
-            for h in range(2):
-                for dist in dists:
+    def sent(r, s, phase):
+        for h in range(2):
+            for dist in dists:
+                if phase == 0:
                     for part in parts1(r, s, h):
                         copy1(r, s, h, part, dist).wait_send()
-                    copy2(r, s, h, dist).wait_send()
-                    copy3(r, s, h, dist).wait_send()
+                else:
+                    (copy2, copy3)[phase - 1](r, s, h, dist).wait_send()
 
     def reduce_rest(r):
+        for phase, finish in enumerate((finish1, finish2, finish3)):
+            if phase == 2:
+                for s in range(2):
+                    sent(r, s, 2)
+            for s in range(2):
+                finish(r, s)
+                if phase < 2:
+                    sent(r, s, phase)
+
+    kept = range(shared, pairs)
+
+    def oth_block():
         for s in range(2):
-            finish1(r, s)
+            take(s)
+        off = coulomb(kept, oth_row, half).T
+        j_acc[...] = coulomb(kept, own_row, half)
         for s in range(2):
-            finish2(r, s)
-        for s in range(2):
-            finish3(r, s)
-        sent(r)
-
-    kept = range(shared, pairs)
-
-    def alpha_oth():
-        take(0)
-        j_t[...] = coulomb(kept, oth_row, half).T
-        j_acc[...] = coulomb(kept, own_row, half)
-        z_f[0] = oth_products(0) - j_t[...]
-
-    def beta_oth():
-        take(1)
-        j_acc[...] = coulomb(range(shared), own_row, half, j_acc)
-        z_f[1] = oth_products(1) - j_t[...]
-
-    def alpha_own():
-        y_acc[...] = own_products(0)
-
-    def beta_own():
-        y_acc[...] = own_products(1)
+            z_f[s] = oth_products(s) - off
+
+    def alpha_block():
+        j_own = coulomb(range(shared), own_row, half, j_acc)
+        j_acc[...] = j_own
+        y = own_products(0)
+        put(0, 0, j_own - (y + y.T))
+
+    def beta_block():
+        y = own_products(1)
+        put(1, 0, j_acc[...] - (y + y.T))
 
     for p in range(shared):
         t_copy(p).wait_recv()
         g_landed(shared + p)
-    block(alpha_oth)
-    z_copy(0).start()
+    block(oth_block)
+    for s in range(2):
+        z_copy(s).start()
     for p in range(shared):
         g_landed(p)
-    block(beta_oth)
-    z_copy(1).start()
-    z_copy(0).wait_recv()
-    put_oth(0)
+    block(alpha_block)
+    by_core(start1, 0, 0)
+    for s in range(2):
+        z_copy(s).wait_recv()
+        put_oth(s)
     by_core(start1, 0, 1)
-    block(alpha_own)
-    put_own(0)
-    by_core(start1, 0, 0)
-    z_copy(1).wait_recv()
-    put_oth(1)
     by_core(start1, 1, 1)
-    block(beta_own)
-    put_own(1)
+    block(beta_block)
     by_core(start1, 1, 0)
-    by_core(reduce_rest)
     for p in range(shared):
         t_copy(p).wait_send()
     for p in range(pairs):
         g_copy(p).wait_send()
     for s in range(2):
         z_copy(s).wait_send()
+    by_core(reduce_rest)
 
 
 def solution(mesh):
@@ -370,8 +365,6 @@
                 vmem((pairs, 2, 8, 128), F32),
                 vmem((pairs, 3, 2, 2, half, 128), BF16),
                 vmem((2, pairs // 2, 3, 2, half, 128), BF16),
-                vmem((half, half), F32),
-                vmem((half, half), F32),
                 vmem((half, half), F32),
                 vmem((2, half, half), F32),
                 vmem((2, half, half), F32),

time: 37.7 us -> 37.1 us (0.984)
  Pallas kernels: 36.3 us -> 35.7 us
    pallas_call x1, Pallas kernels: 36.3 us -> 35.7 us  [local_build(): pl.pallas_call(functools.partial(kernel, n_q, rows), out_shape=pltpu.VMEM...]
where the time goes in v6:
time: 37.1 us; the launch traced here: 37 us
  Pallas kernels  35.7 us (96%)
  between operations  0.64 us (2%)
  local copies, waits for them, and re-layouts  0.61 us (2%)
    pallas_call x1, Pallas kernels, local_build(): pl.pallas_call(functools.partial(kernel, n_q, rows), out_shape=pltpu.VMEM...  35.7 us

profile of v6, /device:TPU:0, one launch (start us, length us, event | category | flops | bytes accessed | tf_op | source)
XLA Modules:
  0.0 37.0 jit_solution(9522217311355396173)
XLA Ops:
  0.6 35.7 %shard_map.50 = f32[2,8,256]{2,1,0:T(8,128)S(1)} custom-call(f32[20,256,512]{2,1,0:T(8,128)} %refs_0_.1, f32[105,512]{1,0:T(8,128)} %bitcast.10, f32[104,512]{1,0:T(8,128)} %bitcast.11), custom_call_target="tpu_custom_call" | custom-call | tf_op jit(solution)/shard_map/pallas_call | solution.py:350
  36.4 0.6 %slice_bitcast_fusion = (f32[256,8]{0,1:T(8,128)}, f32[256,8]{0,1:T(8,128)}) fusion(f32[2,8,256]{2,1,0:T(8,128)S(1)} %shard_map.50), kind=kLoop, calls=%fused_computation | loop fusion | bytes 32768 | tf_op jit(solution)/shard_map/transpose | solution.py:395

commit v7 on v6

--- a/solution.py
+++ b/solution.py
@@ -37,7 +37,7 @@
 
 
 def kernel(n_q, rows, *refs):
-    (b_ref, ca_ref, cb_ref, o_ref, b_v, ca_v, cb_v, c_pad, c_f, c_s, t_f, t_r, g_f, g_r, own, oth, j_acc, z_f, z_r,
+    (b_ref, ca_ref, cb_ref, o_ref, b_v, ca_v, cb_v, c_pad, c_f, c_s, t_f, t_r, g_f, g_r, own, oth, j_acc, j_t, z_f, z_r,
      p_buf, r1, s1, r2, s2, r3, b_sem, c_sem, t_send, t_recv, g_send, g_recv, z_send, z_recv,
      send1, recv1, send2, recv2, send3, recv3) = refs
     pairs = n_q // 2
@@ -296,40 +296,39 @@
 
     kept = range(shared, pairs)
 
-    def oth_block():
-        for s in range(2):
-            take(s)
-        off = coulomb(kept, oth_row, half).T
+    def alpha_oth():
+        take(0)
+        j_t[...] = coulomb(kept, oth_row, half).T
         j_acc[...] = coulomb(kept, own_row, half)
-        for s in range(2):
-            z_f[s] = oth_products(s) - off
-
-    def alpha_block():
-        j_own = coulomb(range(shared), own_row, half, j_acc)
-        j_acc[...] = j_own
-        y = own_products(0)
-        put(0, 0, j_own - (y + y.T))
-
-    def beta_block():
-        y = own_products(1)
-        put(1, 0, j_acc[...] - (y + y.T))
+        z_f[0] = oth_products(0) - j_t[...]
+
+    def beta_oth():
+        take(1)
+        j_acc[...] = coulomb(range(shared), own_row, half, j_acc)
+        z_f[1] = oth_products(1) - j_t[...]
+
+    def own_block(s):
+        y = own_products(s)
+        put(s, 0, j_acc[...] - (y + y.T))
 
     for p in range(shared):
         t_copy(p).wait_recv()
         g_landed(shared + p)
-    block(oth_block)
-    for s in range(2):
-        z_copy(s).start()
+    block(alpha_oth)
+    z_copy(0).start()
     for p in range(shared):
         g_landed(p)
-    block(alpha_block)
+    block(beta_oth)
+    z_copy(1).start()
+    z_copy(0).wait_recv()
+    put_oth(0)
+    by_core(start1, 0, 1)
+    block(functools.partial(own_block, 0))
     by_core(start1, 0, 0)
-    for s in range(2):
-        z_copy(s).wait_recv()
-        put_oth(s)
-    by_core(start1, 0, 1)
+    z_copy(1).wait_recv()
+    put_oth(1)
     by_core(start1, 1, 1)
-    block(beta_block)
+    block(functools.partial(own_block, 1))
     by_core(start1, 1, 0)
     for p in range(shared):
         t_copy(p).wait_send()
@@ -365,6 +364,7 @@
                 vmem((pairs, 2, 8, 128), F32),
                 vmem((pairs, 3, 2, 2, half, 128), BF16),
                 vmem((2, pairs // 2, 3, 2, half, 128), BF16),
+                vmem((half, half), F32),
                 vmem((half, half), F32),
                 vmem((2, half, half), F32),
                 vmem((2, half, half), F32),

time: 37.1 us -> 36.9 us (level)
  no operation moved by 1% of the time
where the time goes in v7:
time: 36.9 us; the launch traced here: 36.8 us
  Pallas kernels  35.5 us (96%)
  between operations  0.64 us (2%)
  local copies, waits for them, and re-layouts  0.61 us (2%)
    pallas_call x1, Pallas kernels, local_build(): pl.pallas_call(functools.partial(kernel, n_q, rows), out_shape=pltpu.VMEM...  35.5 us

profile of v7, /device:TPU:0, one launch (start us, length us, event | category | flops | bytes accessed | tf_op | source)
XLA Modules:
  0.0 36.8 jit_solution(11673275420101985501)
XLA Ops:
  0.6 35.5 %shard_map.50 = f32[2,8,256]{2,1,0:T(8,128)S(1)} custom-call(f32[20,256,512]{2,1,0:T(8,128)} %refs_0_.1, f32[105,512]{1,0:T(8,128)} %bitcast.10, f32[104,512]{1,0:T(8,128)} %bitcast.11), custom_call_target="tpu_custom_call" | custom-call | tf_op jit(solution)/shard_map/pallas_call | solution.py:349
  36.2 0.6 %slice_bitcast_fusion = (f32[256,8]{0,1:T(8,128)}, f32[256,8]{0,1:T(8,128)}) fusion(f32[2,8,256]{2,1,0:T(8,128)S(1)} %shard_map.50), kind=kLoop, calls=%fused_computation | loop fusion | bytes 32768 | tf_op jit(solution)/shard_map/transpose | solution.py:395

commit v8 on v7

--- a/solution.py
+++ b/solution.py
@@ -37,7 +37,7 @@
 
 
 def kernel(n_q, rows, *refs):
-    (b_ref, ca_ref, cb_ref, o_ref, b_v, ca_v, cb_v, c_pad, c_f, c_s, t_f, t_r, g_f, g_r, own, oth, j_acc, j_t, z_f, z_r,
+    (b_ref, ca_ref, cb_ref, o_ref, b_v, ca_v, cb_v, c_pad, c_f, c_s, t_f, t_r, g_f, g_r, own, oth, j_acc, j_t, z_f, z_t, z_r,
      p_buf, r1, s1, r2, s2, r3, b_sem, c_sem, t_send, t_recv, g_send, g_recv, z_send, z_recv,
      send1, recv1, send2, recv2, send3, recv3) = refs
     pairs = n_q // 2
@@ -99,7 +99,7 @@
 
     def z_copy(s):
         return pltpu.make_async_remote_copy(
-            src_ref=z_f.at[s], dst_ref=z_r.at[s], send_sem=z_send.at[s], recv_sem=z_recv.at[s],
+            src_ref=z_t.at[s], dst_ref=z_r.at[s], send_sem=z_send.at[s], recv_sem=z_recv.at[s],
             device_id=partner, device_id_type=MESH)
 
     def t_step(p):
@@ -191,7 +191,7 @@
             p_buf[s, h, z_pair[part]] = block[:, h * 128:(h + 1) * 128].reshape(2, 4, 4, 8, 128)
 
     def put_oth(s):
-        put(s, 1, -(z_f[s] + z_r[s].T))
+        put(s, 1, -(z_f[s] + z_r[s]))
 
     def by_core(body, *args):
         for r in range(2):
@@ -300,12 +300,16 @@
         take(0)
         j_t[...] = coulomb(kept, oth_row, half).T
         j_acc[...] = coulomb(kept, own_row, half)
-        z_f[0] = oth_products(0) - j_t[...]
+        z = oth_products(0) - j_t[...]
+        z_f[0] = z
+        z_t[0] = z.T
 
     def beta_oth():
         take(1)
         j_acc[...] = coulomb(range(shared), own_row, half, j_acc)
-        z_f[1] = oth_products(1) - j_t[...]
+        z = oth_products(1) - j_t[...]
+        z_f[1] = z
+        z_t[1] = z.T
 
     def own_block(s):
         y = own_products(s)
@@ -368,6 +372,7 @@
                 vmem((half, half), F32),
                 vmem((2, half, half), F32),
                 vmem((2, half, half), F32),
+                vmem((2, half, half), F32),
                 vmem((2, 2, 4, 4, 4, 8, 128), F32),
                 vmem((2, 2, 3, 4, 4, 8, 128), F32),
                 vmem((2, 2, 4, 4, 8, 128), F32),

time: 36.9 us -> 36.8 us (level)
  no operation moved by 1% of the time
where the time goes in v8:
time: 36.8 us; the launch traced here: 36.7 us
  Pallas kernels  35.5 us (96%)
  between operations  0.64 us (2%)
  local copies, waits for them, and re-layouts  0.61 us (2%)
    pallas_call x1, Pallas kernels, local_build(): pl.pallas_call(functools.partial(kernel, n_q, rows), out_shape=pltpu.VMEM...  35.5 us

profile of v8, /device:TPU:0, one launch (start us, length us, event | category | flops | bytes accessed | tf_op | source)
XLA Modules:
  0.0 36.7 jit_solution(1400850352032371887)
XLA Ops:
  0.6 35.5 %shard_map.50 = f32[2,8,256]{2,1,0:T(8,128)S(1)} custom-call(f32[20,256,512]{2,1,0:T(8,128)} %refs_0_.1, f32[105,512]{1,0:T(8,128)} %bitcast.10, f32[104,512]{1,0:T(8,128)} %bitcast.11), custom_call_target="tpu_custom_call" | custom-call | tf_op jit(solution)/shard_map/pallas_call | solution.py:353
  36.1 0.6 %slice_bitcast_fusion = (f32[256,8]{0,1:T(8,128)}, f32[256,8]{0,1:T(8,128)}) fusion(f32[2,8,256]{2,1,0:T(8,128)S(1)} %shard_map.50), kind=kLoop, calls=%fused_computation | loop fusion | bytes 32768 | tf_op jit(solution)/shard_map/transpose | solution.py:400
